TPU v7x, 8 devices: a whole 2x2x1 slice. The times are simulated.
8 devices in a mesh: depth: 2 (over z, y), col: 2 (over x), row: 2 (over core).
Axes of the slice: x: 2, y: 2, z: 1, core: 2. Of those that a mesh axis runs over, the one named last changes fastest.
Arguments:
- reach_in: bfloat16 [7168, 7168], P(('row', 'depth'), 'col')
Outputs:
- output: bfloat16 [7168, 7168], P(('row', 'depth'), 'col')
All inputs are finite; a program needn't handle non-finite values.
Results may differ from a plain program's by a relative error of at most 0.001.
Values are sent between devices in bfloat16 or wider.
A program may use at most 1 GiB of HBM per device.

v0:
```python
import jax
import jax.numpy as jnp
from jax import lax
from jax.sharding import PartitionSpec as P

SQUARINGS = 4


def solution(mesh):
    depth_size = mesh.shape['depth']
    col_size = mesh.shape['col']
    row_size = mesh.shape['row']
    col_ratio = row_size // col_size
    per_layer = row_size // depth_size
    n_used = min(col_ratio, per_layer)
    all_axes = ('depth', 'col', 'row')

    def linear(layer_id, col_id, row_id):
        return (layer_id * col_size + col_id) * row_size + row_id

    def a_perm(piece_id):
        perm_pairs = []
        for layer_id in range(depth_size):
            for col_id in range(col_size):
                for row_id in range(row_size):
                    offset = (row_id + layer_id * per_layer + piece_id) // col_ratio
                    perm_pairs.append((linear(layer_id, col_id, row_id), linear(layer_id, (col_id - offset) % col_size, row_id)))
        return perm_pairs

    def b_perm():
        perm_pairs = []
        for layer_id in range(depth_size):
            for col_id in range(col_size):
                for k_id in range(row_size):
                    dest_row = (k_id - col_id * col_ratio - layer_id * per_layer) % row_size
                    perm_pairs.append((linear(layer_id, col_id, k_id), linear(layer_id, col_id, dest_row)))
        return perm_pairs

    a_perms = [a_perm(piece_id) for piece_id in range(n_used)]
    b_skew = b_perm()
    col_shift = [(col_id, (col_id - 1) % col_size) for col_id in range(col_size)]
    row_shift = [(row_id, (row_id - 1) % row_size) for row_id in range(row_size)]

    def local_squarings(row_slab):
        row_idx = lax.axis_index('row')
        layer_idx = lax.axis_index('depth')
        for _ in range(SQUARINGS):
            full_block = lax.all_gather(row_slab, 'depth', axis=0, tiled=True)
            k_width = full_block.shape[0]
            window = []
            for piece_id in range(n_used):
                if col_ratio == 1:
                    a_piece = full_block
                else:
                    sub_idx = (row_idx + layer_idx * per_layer + piece_id) % col_ratio
                    a_piece = lax.dynamic_slice_in_dim(full_block, sub_idx * k_width, k_width, axis=1)
                window.append(lax.ppermute(a_piece, all_axes, a_perms[piece_id]))
            b_block = lax.ppermute(full_block, all_axes, b_skew)
            partial_sum = None
            for step_id in range(per_layer):
                slot_id = step_id % col_ratio
                product = jnp.dot(window[slot_id], b_block, preferred_element_type=jnp.float32)
                partial_sum = product if partial_sum is None else partial_sum + product
                if step_id + col_ratio < per_layer:
                    window[slot_id] = lax.ppermute(window[slot_id], 'col', col_shift)
                if step_id + 1 < per_layer:
                    b_block = lax.ppermute(b_block, 'row', row_shift)
            reduced = lax.psum_scatter(partial_sum, 'depth', scatter_dimension=0, tiled=True)
            row_slab = jnp.minimum(reduced + row_slab.astype(jnp.float32), 1.0).astype(jnp.bfloat16)
        return row_slab

    layout = P(('row', 'depth'), 'col')
    return jax.shard_map(local_squarings, mesh=mesh, in_specs=(layout,), out_specs=layout, check_vma=False)
```

profile of v0, /device:TPU:0, one launch (start us, length us, event | category | flops | bytes accessed | tf_op | source)
XLA Modules:
  0.0 5828.4 jit_solution(9623501393235134288)
XLA Ops:
  6.5 0.0 all-gather.5.cloned.1.call-start
  6.5 0.7 all-gather.5.cloned.1.call-update
  7.3 0.0 reduce-scatter.13.cloned.1.call-start
  7.3 303.5 %all-gather.5.cloned.1.call-done = bf16[3584,3584]{1,0:T(8,128)(2,1)} async-done(((bf16[1792,3584]{1,0:T(8,128)(2,1)}), bf16[3584,3584]{1,0:T(8,128)(2,1)}) %all-gather.5.cloned.1.call-update) | async-done | bytes 25690128 | tf_op jit(solution)/shard_map/all_gather | solution.py:48
  310.8 194.1 %collective-permute-start.1 = (bf16[3584,3584]{1,0:T(8,128)(2,1)}, bf16[3584,3584]{1,0:T(8,128)(2,1)}, u32[]{:S(2)}, u32[]{:S(2)}) collective-permute-start(bf16[3584,3584]{1,0:T(8,128)(2,1)} %all-gather.5.cloned.1.call-done), channel_id=1, source_target_pairs={{0,0},{1,1},{2,3},{3,2},{4,5},{5,4},{6,6},{7,7}} | collective-permute-start | bytes 77070344 | tf_op jit(solution)/shard_map/ppermute | solution.py:58
  504.9 194.1 %collective-permute-start = (bf16[3584,3584]{1,0:T(8,128)(2,1)}, bf16[3584,3584]{1,0:T(8,128)(2,1)}, u32[]{:S(2)}, u32[]{:S(2)}) collective-permute-start(bf16[3584,3584]{1,0:T(8,128)(2,1)} %all-gather.5.cloned.1.call-done), channel_id=1, source_target_pairs={{0,0},{1,3},{2,2},{3,1},{4,6},{5,5},{6,4},{7,7}} | collective-permute-start | bytes 77070344 | tf_op jit(solution)/shard_map/ppermute | solution.py:57
  699.0 0.0 collective-permute-done.1
  699.0 0.0 collective-permute-done
  699.0 103.3 %fusion = f32[3584,3584]{1,0:T(8,128)} fusion(bf16[3584,3584]{1,0:T(8,128)(2,1)} %collective-permute-done, bf16[3584,3584]{1,0:T(8,128)(2,1)} %collective-permute-done.1), kind=kOutput, calls=%fused_computation.4 | convolution fusion | flops 92073361408 | bytes 102760448 | tf_op jit(solution)/shard_map/dot_general | solution.py:62
  802.3 0.0 reduce-scatter.13.cloned.1.call-update
  802.4 0.0 all-gather.7.cloned.1.call-start
  802.4 644.1 %reduce-scatter.13.cloned.1.call-done = f32[1792,3584]{1,0:T(8,128)} async-done(((f32[3584,3584]{1,0:T(8,128)}), f32[1792,3584]{1,0:T(8,128)}) %reduce-scatter.13.cloned.1.call-update) | async-done | bytes 25690128
  1446.5 17.5 minimum_convert_fusion.3
  1464.0 0.0 all-gather.7.cloned.1.call-update
  1464.1 0.0 reduce-scatter.15.cloned.1.call-start
  1464.1 299.2 %all-gather.7.cloned.1.call-done = bf16[3584,3584]{1,0:T(8,128)(2,1)} async-done(((bf16[1792,3584]{1,0:T(8,128)(2,1)}), bf16[3584,3584]{1,0:T(8,128)(2,1)}) %all-gather.7.cloned.1.call-update) | async-done | bytes 25690128 | tf_op jit(solution)/shard_map/all_gather | solution.py:48
  1763.3 194.1 %collective-permute-start.3 = (bf16[3584,3584]{1,0:T(8,128)(2,1)}, bf16[3584,3584]{1,0:T(8,128)(2,1)}, u32[]{:S(2)}, u32[]{:S(2)}) collective-permute-start(bf16[3584,3584]{1,0:T(8,128)(2,1)} %all-gather.7.cloned.1.call-done), channel_id=1, source_target_pairs={{0,0},{1,1},{2,3},{3,2},{4,5},{5,4},{6,6},{7,7}} | collective-permute-start | bytes 77070344 | tf_op jit(solution)/shard_map/ppermute | solution.py:58
  1957.4 194.1 %collective-permute-start.2 = (bf16[3584,3584]{1,0:T(8,128)(2,1)}, bf16[3584,3584]{1,0:T(8,128)(2,1)}, u32[]{:S(2)}, u32[]{:S(2)}) collective-permute-start(bf16[3584,3584]{1,0:T(8,128)(2,1)} %all-gather.7.cloned.1.call-done), channel_id=1, source_target_pairs={{0,0},{1,3},{2,2},{3,1},{4,6},{5,5},{6,4},{7,7}} | collective-permute-start | bytes 77070344 | tf_op jit(solution)/shard_map/ppermute | solution.py:57
  2151.5 0.0 collective-permute-done.3
  2151.5 0.0 collective-permute-done.2
  2151.5 103.3 %fusion.1 = f32[3584,3584]{1,0:T(8,128)} fusion(bf16[3584,3584]{1,0:T(8,128)(2,1)} %collective-permute-done.2, bf16[3584,3584]{1,0:T(8,128)(2,1)} %collective-permute-done.3), kind=kOutput, calls=%fused_computation.5 | convolution fusion | flops 92073361408 | bytes 102760448 | tf_op jit(solution)/shard_map/dot_general | solution.py:62
  2254.9 0.0 reduce-scatter.15.cloned.1.call-update
  2254.9 0.0 all-gather.9.cloned.1.call-start
  2254.9 644.1 %reduce-scatter.15.cloned.1.call-done = f32[1792,3584]{1,0:T(8,128)} async-done(((f32[3584,3584]{1,0:T(8,128)}), f32[1792,3584]{1,0:T(8,128)}) %reduce-scatter.15.cloned.1.call-update) | async-done | bytes 25690128
  2899.1 17.5 minimum_convert_fusion.2
  2916.6 0.0 all-gather.9.cloned.1.call-update
  2916.6 0.0 reduce-scatter.17.cloned.1.call-start
  2916.6 299.2 %all-gather.9.cloned.1.call-done = bf16[3584,3584]{1,0:T(8,128)(2,1)} async-done(((bf16[1792,3584]{1,0:T(8,128)(2,1)}), bf16[3584,3584]{1,0:T(8,128)(2,1)}) %all-gather.9.cloned.1.call-update) | async-done | bytes 25690128 | tf_op jit(solution)/shard_map/all_gather | solution.py:48
  3215.9 194.1 %collective-permute-start.5 = (bf16[3584,3584]{1,0:T(8,128)(2,1)}, bf16[3584,3584]{1,0:T(8,128)(2,1)}, u32[]{:S(2)}, u32[]{:S(2)}) collective-permute-start(bf16[3584,3584]{1,0:T(8,128)(2,1)} %all-gather.9.cloned.1.call-done), channel_id=1, source_target_pairs={{0,0},{1,1},{2,3},{3,2},{4,5},{5,4},{6,6},{7,7}} | collective-permute-start | bytes 77070344 | tf_op jit(solution)/shard_map/ppermute | solution.py:58
  3409.9 194.1 %collective-permute-start.4 = (bf16[3584,3584]{1,0:T(8,128)(2,1)}, bf16[3584,3584]{1,0:T(8,128)(2,1)}, u32[]{:S(2)}, u32[]{:S(2)}) collective-permute-start(bf16[3584,3584]{1,0:T(8,128)(2,1)} %all-gather.9.cloned.1.call-done), channel_id=1, source_target_pairs={{0,0},{1,3},{2,2},{3,1},{4,6},{5,5},{6,4},{7,7}} | collective-permute-start | bytes 77070344 | tf_op jit(solution)/shard_map/ppermute | solution.py:57
  3604.0 0.0 collective-permute-done.5
  3604.0 0.0 collective-permute-done.4
  3604.0 103.3 %fusion.2 = f32[3584,3584]{1,0:T(8,128)} fusion(bf16[3584,3584]{1,0:T(8,128)(2,1)} %collective-permute-done.4, bf16[3584,3584]{1,0:T(8,128)(2,1)} %collective-permute-done.5), kind=kOutput, calls=%fused_computation.6 | convolution fusion | flops 92073361408 | bytes 102760448 | tf_op jit(solution)/shard_map/dot_general | solution.py:62
  3707.4 0.0 reduce-scatter.17.cloned.1.call-update
  3707.4 0.0 all-gather.11.cloned.1.call-start
  3707.4 644.1 %reduce-scatter.17.cloned.1.call-done = f32[1792,3584]{1,0:T(8,128)} async-done(((f32[3584,3584]{1,0:T(8,128)}), f32[1792,3584]{1,0:T(8,128)}) %reduce-scatter.17.cloned.1.call-update) | async-done | bytes 25690128
  4351.6 17.5 minimum_convert_fusion.1
  4369.1 0.0 all-gather.11.cloned.1.call-update
  4369.1 0.0 reduce-scatter.19.cloned.1.call-start
  4369.1 299.2 %all-gather.11.cloned.1.call-done = bf16[3584,3584]{1,0:T(8,128)(2,1)} async-done(((bf16[1792,3584]{1,0:T(8,128)(2,1)}), bf16[3584,3584]{1,0:T(8,128)(2,1)}) %all-gather.11.cloned.1.call-update) | async-done | bytes 25690128 | tf_op jit(solution)/shard_map/all_gather | solution.py:48
  4668.4 194.1 %collective-permute-start.7 = (bf16[3584,3584]{1,0:T(8,128)(2,1)}, bf16[3584,3584]{1,0:T(8,128)(2,1)}, u32[]{:S(2)}, u32[]{:S(2)}) collective-permute-start(bf16[3584,3584]{1,0:T(8,128)(2,1)} %all-gather.11.cloned.1.call-done), channel_id=1, source_target_pairs={{0,0},{1,1},{2,3},{3,2},{4,5},{5,4},{6,6},{7,7}} | collective-permute-start | bytes 77070344 | tf_op jit(solution)/shard_map/ppermute | solution.py:58
  4862.4 194.1 %collective-permute-start.6 = (bf16[3584,3584]{1,0:T(8,128)(2,1)}, bf16[3584,3584]{1,0:T(8,128)(2,1)}, u32[]{:S(2)}, u32[]{:S(2)}) collective-permute-start(bf16[3584,3584]{1,0:T(8,128)(2,1)} %all-gather.11.cloned.1.call-done), channel_id=1, source_target_pairs={{0,0},{1,3},{2,2},{3,1},{4,6},{5,5},{6,4},{7,7}} | collective-permute-start | bytes 77070344 | tf_op jit(solution)/shard_map/ppermute | solution.py:57
  5056.5 0.0 collective-permute-done.7
  5056.5 0.0 collective-permute-done.6
  5056.5 103.3 %fusion.3 = f32[3584,3584]{1,0:T(8,128)} fusion(bf16[3584,3584]{1,0:T(8,128)(2,1)} %collective-permute-done.6, bf16[3584,3584]{1,0:T(8,128)(2,1)} %collective-permute-done.7), kind=kOutput, calls=%fused_computation.7 | convolution fusion | flops 92073361408 | bytes 102760448 | tf_op jit(solution)/shard_map/dot_general | solution.py:62
  5159.9 0.0 reduce-scatter.19.cloned.1.call-update
  5159.9 644.2 %reduce-scatter.19.cloned.1.call-done = f32[1792,3584]{1,0:T(8,128)} async-done(((f32[3584,3584]{1,0:T(8,128)}), f32[1792,3584]{1,0:T(8,128)}) %reduce-scatter.19.cloned.1.call-update) | async-done | bytes 25690128
  5804.1 17.5 minimum_convert_fusion
Async XLA Ops:
  6.5 304.3 %all-gather.5.cloned.1.call-start = ((), (), s32[]{:S(2)}) async-start(), calls=%async_computation.4 | async-start | bytes 38535168 | tf_op jit(solution)/shard_map/all_gather | solution.py:48
  7.3 1439.3 %reduce-scatter.13.cloned.1.call-start = ((), (), s32[]{:S(2)}) async-start(), calls=%async_computation.8 | async-start | bytes 77070336
  310.8 388.2 %collective-permute-start.1 = (bf16[3584,3584]{1,0:T(8,128)(2,1)}, bf16[3584,3584]{1,0:T(8,128)(2,1)}, u32[]{:S(2)}, u32[]{:S(2)}) collective-permute-start(bf16[3584,3584]{1,0:T(8,128)(2,1)} %all-gather.5.cloned.1.call-done), channel_id=1, source_target_pairs={{0,0},{1,1},{2,3},{3,2},{4,5},{5,4},{6,6},{7,7}} | collective-permute-start | bytes 77070344 | tf_op jit(solution)/shard_map/ppermute | solution.py:58
  504.9 194.1 %collective-permute-start = (bf16[3584,3584]{1,0:T(8,128)(2,1)}, bf16[3584,3584]{1,0:T(8,128)(2,1)}, u32[]{:S(2)}, u32[]{:S(2)}) collective-permute-start(bf16[3584,3584]{1,0:T(8,128)(2,1)} %all-gather.5.cloned.1.call-done), channel_id=1, source_target_pairs={{0,0},{1,3},{2,2},{3,1},{4,6},{5,5},{6,4},{7,7}} | collective-permute-start | bytes 77070344 | tf_op jit(solution)/shard_map/ppermute | solution.py:57
  802.4 961.0 %all-gather.7.cloned.1.call-start = ((), (), s32[]{:S(2)}) async-start(), calls=%async_computation.5 | async-start | bytes 38535168 | tf_op jit(solution)/shard_map/all_gather | solution.py:48
  1464.1 1435.0 %reduce-scatter.15.cloned.1.call-start = ((), (), s32[]{:S(2)}) async-start(), calls=%async_computation.9 | async-start | bytes 77070336
  1763.3 388.2 %collective-permute-start.3 = (bf16[3584,3584]{1,0:T(8,128)(2,1)}, bf16[3584,3584]{1,0:T(8,128)(2,1)}, u32[]{:S(2)}, u32[]{:S(2)}) collective-permute-start(bf16[3584,3584]{1,0:T(8,128)(2,1)} %all-gather.7.cloned.1.call-done), channel_id=1, source_target_pairs={{0,0},{1,1},{2,3},{3,2},{4,5},{5,4},{6,6},{7,7}} | collective-permute-start | bytes 77070344 | tf_op jit(solution)/shard_map/ppermute | solution.py:58
  1957.4 194.1 %collective-permute-start.2 = (bf16[3584,3584]{1,0:T(8,128)(2,1)}, bf16[3584,3584]{1,0:T(8,128)(2,1)}, u32[]{:S(2)}, u32[]{:S(2)}) collective-permute-start(bf16[3584,3584]{1,0:T(8,128)(2,1)} %all-gather.7.cloned.1.call-done), channel_id=1, source_target_pairs={{0,0},{1,3},{2,2},{3,1},{4,6},{5,5},{6,4},{7,7}} | collective-permute-start | bytes 77070344 | tf_op jit(solution)/shard_map/ppermute | solution.py:57
  2254.9 961.0 %all-gather.9.cloned.1.call-start = ((), (), s32[]{:S(2)}) async-start(), calls=%async_computation.6 | async-start | bytes 38535168 | tf_op jit(solution)/shard_map/all_gather | solution.py:48
  2916.6 1435.0 %reduce-scatter.17.cloned.1.call-start = ((), (), s32[]{:S(2)}) async-start(), calls=%async_computation.10 | async-start | bytes 77070336
  3215.9 388.2 %collective-permute-start.5 = (bf16[3584,3584]{1,0:T(8,128)(2,1)}, bf16[3584,3584]{1,0:T(8,128)(2,1)}, u32[]{:S(2)}, u32[]{:S(2)}) collective-permute-start(bf16[3584,3584]{1,0:T(8,128)(2,1)} %all-gather.9.cloned.1.call-done), channel_id=1, source_target_pairs={{0,0},{1,1},{2,3},{3,2},{4,5},{5,4},{6,6},{7,7}} | collective-permute-start | bytes 77070344 | tf_op jit(solution)/shard_map/ppermute | solution.py:58
  3409.9 194.1 %collective-permute-start.4 = (bf16[3584,3584]{1,0:T(8,128)(2,1)}, bf16[3584,3584]{1,0:T(8,128)(2,1)}, u32[]{:S(2)}, u32[]{:S(2)}) collective-permute-start(bf16[3584,3584]{1,0:T(8,128)(2,1)} %all-gather.9.cloned.1.call-done), channel_id=1, source_target_pairs={{0,0},{1,3},{2,2},{3,1},{4,6},{5,5},{6,4},{7,7}} | collective-permute-start | bytes 77070344 | tf_op jit(solution)/shard_map/ppermute | solution.py:57
  3707.4 961.0 %all-gather.11.cloned.1.call-start = ((), (), s32[]{:S(2)}) async-start(), calls=%async_computation.7 | async-start | bytes 38535168 | tf_op jit(solution)/shard_map/all_gather | solution.py:48
  4369.1 1435.0 %reduce-scatter.19.cloned.1.call-start = ((), (), s32[]{:S(2)}) async-start(), calls=%async_computation.11 | async-start | bytes 77070336
  4668.4 388.2 %collective-permute-start.7 = (bf16[3584,3584]{1,0:T(8,128)(2,1)}, bf16[3584,3584]{1,0:T(8,128)(2,1)}, u32[]{:S(2)}, u32[]{:S(2)}) collective-permute-start(bf16[3584,3584]{1,0:T(8,128)(2,1)} %all-gather.11.cloned.1.call-done), channel_id=1, source_target_pairs={{0,0},{1,1},{2,3},{3,2},{4,5},{5,4},{6,6},{7,7}} | collective-permute-start | bytes 77070344 | tf_op jit(solution)/shard_map/ppermute | solution.py:58
  4862.4 194.1 %collective-permute-start.6 = (bf16[3584,3584]{1,0:T(8,128)(2,1)}, bf16[3584,3584]{1,0:T(8,128)(2,1)}, u32[]{:S(2)}, u32[]{:S(2)}) collective-permute-start(bf16[3584,3584]{1,0:T(8,128)(2,1)} %all-gather.11.cloned.1.call-done), channel_id=1, source_target_pairs={{0,0},{1,3},{2,2},{3,1},{4,6},{5,5},{6,4},{7,7}} | collective-permute-start | bytes 77070344 | tf_op jit(solution)/shard_map/ppermute | solution.py:57
Sparse Core Ops, SparseCore 0:
  8.9 301.9 all-gather.4
  802.5 644.0 reduce-scatter.12
  1464.2 299.1 all-gather.6
  2255.0 644.0 reduce-scatter.14
  2916.7 299.1 all-gather.8
  3707.5 644.0 reduce-scatter.16
  4369.2 299.1 all-gather.10
  5160.0 644.0 reduce-scatter.18
where the time goes:
time: 5940 us; the launch traced here: 5830 us
  waiting for transfers between devices  3780 us (64%)
  starting transfers between devices  1550 us (26%)
  matrix products  413 us (7%)
  other arithmetic  70 us (1%)
    unnamed x12, waiting for transfers between devices  2580 us
    all_gather x4, waiting for transfers between devices, local_squarings(): full_block = lax.all_gather(row_slab, 'depth', axis=0, tiled=True)  1200 us
    ppermute x4, starting transfers between devices, local_squarings(): b_block = lax.ppermute(full_block, all_axes, b_skew)  776 us
    ppermute x4, starting transfers between devices, local_squarings(): window.append(lax.ppermute(a_piece, all_axes, a_perms[piece_id]))  776 us
    dot_general x4, matrix products, local_squarings(): jnp.dot(window[slot_id], b_block, preferred_element_type=jnp.float32)  413 us
  transfers between devices with their start and end apart: 16, of which 8 were waited for; matrix products, arithmetic and copies ran while one was open for 0% of the time, Pallas kernels for 0%

commit v1 on v0

v1 whole, which is shorter than its diff:
```python
import functools

import jax
import jax.numpy as jnp
from jax import lax
from jax.experimental import pallas as pl
from jax.experimental.pallas import tpu as pltpu
from jax.sharding import PartitionSpec as P

SQUARINGS = 4
UNIT = 128
TILE_N = 512
MESH = pl.DeviceIdType.MESH
OWN, PARTNER, VERT, PARTNER_VERT, HORI = range(5)


def chunk_plan(quarter):
    units = quarter // UNIT
    widths = [2] * (units // 2 - 1) + [1, 1]
    plan = []
    start = 0
    local_start = 0
    for c, w in enumerate(widths):
        if c == len(widths) - 1:
            lw = 0
        else:
            lw = 2
        plan.append((start * UNIT, w * UNIT, local_start * UNIT, lw * UNIT))
        start += w
        local_start += lw
    assert start == units and local_start == units
    return plan


def kernel(plan, in_ref, out_ref, work, acc, a_buf, b_buf, stage, x_send, x_recv, y_send, y_recv, p_send, p_recv, r_send,
           r_recv, a_sem, b_sem, o_sem):
    depth = lax.axis_index('depth')
    col = lax.axis_index('col')
    row = lax.axis_index('row')
    rows, cols = in_ref.shape
    quarter = cols // 2
    tiles = cols // TILE_N
    n_chunks = len(plan)
    x_dev = {'col': 1 - col}
    y_dev = {'depth': 1 - depth}
    p_dev = {'row': 1 - row}
    differ = lax.rem(row + col, 2)
    near = pl.multiple_of(depth * quarter, UNIT)
    far = pl.multiple_of((1 - depth) * quarter, UNIT)

    barrier = pltpu.get_barrier_semaphore()
    for dev in (x_dev, y_dev, p_dev):
        pl.semaphore_signal(barrier, inc=1, device_id=dev, device_id_type=MESH)
    pl.semaphore_wait(barrier, 3)

    def remote(src, dst, s_sem, r_sem, dev):
        return pltpu.make_async_remote_copy(src_ref=src, dst_ref=dst, send_sem=s_sem, recv_sem=r_sem, device_id=dev,
                                            device_id_type=MESH)

    def sends(source, par, c):
        start, width, lstart, lwidth = plan[c]
        piece = source.at[pl.ds(start, width), :]
        out = [remote(piece, work.at[par, VERT, pl.ds(start, width), :], y_send.at[par, c], y_recv.at[par, c], y_dev)]
        for h, base in enumerate((near, far)):
            where = pl.ds(pl.multiple_of(base + start, UNIT), width)
            out.append(remote(source.at[:, where], work.at[par, HORI, :, where], x_send.at[par, c, h],
                              x_recv.at[par, c, h], x_dev))
        if lwidth:
            local = pl.ds(lstart, lwidth)
            out.append(remote(source.at[local, :], work.at[par, PARTNER, local, :], p_send.at[par, c],
                              p_recv.at[par, c], p_dev))
        return out

    def relay(par, c):
        start, width, _, _ = plan[c]
        return remote(work.at[par, VERT, pl.ds(start, width), :], work.at[par, PARTNER_VERT, pl.ds(start, width), :],
                      r_send.at[par, c], r_recv.at[par, c], p_dev)

    def start_all(source, par):
        for c in range(n_chunks):
            for copy in sends(source, par, c):
                copy.start()

    start_all(in_ref, 0)

    @pl.loop(0, tiles)
    def _(n):
        where = pl.ds(pl.multiple_of(n * TILE_N, TILE_N), TILE_N)
        load = pltpu.make_async_copy(in_ref.at[:, where], stage.at[0], o_sem.at[0])
        load.start()
        load.wait()
        acc[n] = stage[0].astype(jnp.float32)
        store = pltpu.make_async_copy(stage.at[0], work.at[0, OWN, :, where], o_sem.at[0])
        store.start()
        store.wait()

    def squaring(t, carry):
        par = lax.rem(t, 2)

        @pl.when(t > 0)
        def _():
            start_all(work.at[par, OWN], par)

        for c in range(n_chunks):
            start, width, lstart, lwidth = plan[c]
            last = c == n_chunks - 1
            own_sends = sends(work.at[par, OWN], par, c)
            for copy in own_sends[1:] + own_sends[:1]:
                copy.wait_recv()
            pass_on = relay(par, c)
            pass_on.start()
            pass_on.wait_recv()
            pieces = []
            if lwidth:
                pieces.append((OWN, near, lstart, lwidth, OWN + differ))
            pieces.append((OWN, far, start, width, VERT + differ))
            pieces.append((HORI, near, start, width, PARTNER - differ))
            pieces.append((HORI, far, start, width, PARTNER_VERT - differ))
            offset = 0
            loads = []
            for k, (a_slot, base, s, w, b_slot) in enumerate(pieces):
                where = pl.ds(pl.multiple_of(base + s, UNIT), w)
                loads.append(pltpu.make_async_copy(work.at[par, a_slot, :, where], a_buf.at[:, pl.ds(offset, w)],
                                                   a_sem.at[k]))
                loads.append(pltpu.make_async_copy(work.at[par, b_slot, pl.ds(s, w), :], b_buf.at[pl.ds(offset, w), :],
                                                   b_sem.at[k]))
                offset += w
            for copy in loads:
                copy.start()
            for copy in loads:
                copy.wait()
            width_k = offset

            if not last:
                @pl.loop(0, tiles)
                def _(n):
                    where = pl.ds(pl.multiple_of(n * TILE_N, TILE_N), TILE_N)
                    acc[n] += jnp.dot(a_buf[:, :width_k], b_buf[:width_k, where], preferred_element_type=jnp.float32)
            else:
                def store(n, slot, dst):
                    where = pl.ds(pl.multiple_of(n * TILE_N, TILE_N), TILE_N)
                    return pltpu.make_async_copy(stage.at[slot], dst.at[:, where], o_sem.at[slot])

                def finish(n, carry):
                    where = pl.ds(pl.multiple_of(n * TILE_N, TILE_N), TILE_N)
                    slot = lax.rem(n, 2)

                    @pl.when(n >= 2)
                    def _():
                        store(n, slot, out_ref).wait()

                    product = jnp.dot(a_buf[:, :width_k], b_buf[:width_k, where], preferred_element_type=jnp.float32)
                    fresh = jnp.minimum(acc[n] + product, 1.0)
                    acc[n] = fresh
                    stage[slot] = fresh.astype(jnp.bfloat16)

                    @pl.when(t == SQUARINGS - 1)
                    def _():
                        store(n, slot, out_ref).start()

                    @pl.when(t < SQUARINGS - 1)
                    def _():
                        store(n, slot, work.at[1 - par, OWN]).start()

                    return carry

                lax.fori_loop(0, tiles, finish, 0)
                for n in (tiles - 2, tiles - 1):
                    store(n, n % 2, out_ref).wait()

        for c in range(n_chunks):
            for copy in sends(work.at[par, OWN], par, c):
                copy.wait_send()
            relay(par, c).wait_send()
        return carry

    lax.fori_loop(0, SQUARINGS, squaring, 0)


def solution(mesh):
    def run(slab):
        rows, cols = slab.shape
        plan = chunk_plan(cols // 2)
        n_chunks = len(plan)
        k_max = max(3 * w + lw for _, w, _, lw in plan)
        dma = pltpu.SemaphoreType.DMA
        out, _ = pl.pallas_call(
            functools.partial(kernel, plan),
            out_shape=(jax.ShapeDtypeStruct((rows, cols), jnp.bfloat16),
                       jax.ShapeDtypeStruct((2, 5, rows, cols), jnp.bfloat16)),
            in_specs=[pl.BlockSpec(memory_space=pl.ANY)],
            out_specs=(pl.BlockSpec(memory_space=pl.ANY), pl.BlockSpec(memory_space=pl.ANY)),
            scratch_shapes=[
                pltpu.VMEM((cols // TILE_N, rows, TILE_N), jnp.float32),
                pltpu.VMEM((rows, k_max), jnp.bfloat16),
                pltpu.VMEM((k_max, cols), jnp.bfloat16),
                pltpu.VMEM((2, rows, TILE_N), jnp.bfloat16),
                dma((2, n_chunks, 2)), dma((2, n_chunks, 2)),
                dma((2, n_chunks)), dma((2, n_chunks)),
                dma((2, n_chunks)), dma((2, n_chunks)),
                dma((2, n_chunks)), dma((2, n_chunks)),
                dma((4,)), dma((4,)), dma((2,)),
            ],
            compiler_params=pltpu.CompilerParams(collective_id=0, has_side_effects=True,
                                                 vmem_limit_bytes=67_000_000),
            name='reach_squarings',
        )(slab)
        return out

    layout = P(('row', 'depth'), 'col')
    return jax.shard_map(run, mesh=mesh, in_specs=(layout,), out_specs=layout, check_vma=False)
```

time: 5940 us -> 1180 us (0.20); the launches traced: 5830 us -> 1180 us
  waiting for transfers between devices: 3780 us -> 0 us
  starting transfers between devices: 1550 us -> 0 us
  Pallas kernels: 0 us -> 1170 us
  matrix products: 413 us -> 0 us
  other arithmetic: 70 us -> 0 us
    unnamed x12 -> x0, waiting for transfers between devices: 2580 us -> none
    ppermute x8 -> x0, starting transfers between devices: 1550 us -> none  [the longest x4 776 us: local_squarings(): b_block = lax.ppermute(full_block, all_axes, b_skew)]
    all_gather x4 -> x0, waiting for transfers between devices: 1200 us -> none  [local_squarings(): full_block = lax.all_gather(row_slab, 'depth', axis=0, tiled=True)]
    pallas_call x0 -> x1, Pallas kernels: none -> 1170 us  [run(): pl.pallas_call(functools.partial(kernel, plan), out_shape=(jax.ShapeDtype...]
    dot_general x4 -> x0, matrix products: 413 us -> none  [local_squarings(): jnp.dot(window[slot_id], b_block, preferred_element_type=jnp.float32)]
    convert_element_type x4 -> x0, other arithmetic: 70 us -> none  [local_squarings(): jnp.minimum(reduced + row_slab.astype(jnp.float32), 1.0)]
  transfers between devices with their start and end apart: 16 -> 0, of which waited for: 8 -> 0; matrix products, arithmetic and copies ran while one was open for 0% -> 0% of each run, Pallas kernels for 0% -> 0%
where the time goes in v1:
time: 1180 us
  Pallas kernels  1170 us (99%)
    pallas_call x1, Pallas kernels, run(): pl.pallas_call(functools.partial(kernel, plan), out_shape=(jax.ShapeDtype...  1170 us

profile of v1, /device:TPU:0, one launch (start us, length us, event | category | flops | bytes accessed | tf_op | source)
XLA Modules:
  0.0 1180.3 jit_solution(4289178642678940047)
XLA Ops:
  0.0 1169.7 %reach_squarings.1 = (bf16[1792,3584]{1,0:T(8,128)(2,1)}, bf16[2,5,1792,3584]{3,2,1,0:T(8,128)(2,1)}) custom-call(bf16[1792,3584]{1,0:T(8,128)(2,1)} %in_ref.1), custom_call_target="tpu_custom_call" | custom-call | tf_op jit(solution)/shard_map/reach_squarings/pallas_call | solution.py:187
  1169.7 10.6 copy.3

commit v2 on v0

v2 whole, which is shorter than its diff:
```python
import functools

import jax
import jax.numpy as jnp
from jax import lax
from jax.experimental import pallas as pl
from jax.experimental.pallas import tpu as pltpu
from jax.sharding import PartitionSpec as P

SQUARINGS = 4
SUB = 256
TILE = 512
BLOCK = 448
RING = 3
MESH = pl.DeviceIdType.MESH
OWN, MATE, VERT, MATE_VERT, HORI, MATE_HORI, DIAG, MATE_DIAG = range(8)
LEFT_O = (OWN, HORI)
LEFT_Y = (VERT, DIAG)


class Place:
    def __init__(self, half):
        self.depth = lax.axis_index('depth')
        self.col = lax.axis_index('col')
        self.row = lax.axis_index('row')
        self.differ = lax.rem(self.row + self.col, 2)
        self.half = half
        self.per = half // SUB

    def base(self, f):
        return pl.multiple_of((self.depth + f - 2 * self.depth * f) * self.half, SUB)

    def cols(self, r):
        f, q = r // self.per, r % self.per
        return pl.ds(pl.multiple_of((self.depth + f - 2 * self.depth * f) * self.half + q * SUB, SUB), SUB)

    def rows(self, q):
        return pl.ds(pl.multiple_of(q * SUB, SUB), SUB)

    def right_slot(self, base, h, f):
        return base + 2 * f + (self.differ if h == 0 else 1 - self.differ)


class Engine:
    def __init__(self, place, a_buf, b_buf, acc, ring, eye, a_sem, b_sem, out_sem):
        self.place, self.a_buf, self.b_buf, self.acc, self.ring, self.eye = place, a_buf, b_buf, acc, ring, eye
        self.a_sem, self.b_sem, self.out_sem = a_sem, b_sem, out_sem
        down = lax.broadcasted_iota(jnp.int32, eye.shape, 0)
        across = lax.broadcasted_iota(jnp.int32, eye.shape, 1)
        eye[...] = (down == across).astype(jnp.float32).astype(jnp.bfloat16)

    def load(self, src, slot, lefts, rights, tile0, nt, full):
        p = self.place
        for e in range(2):
            a_slot, r = lefts[e]
            pltpu.make_async_copy(src.at[a_slot, :, p.cols(r)], self.a_buf.at[slot, :, pl.ds(e * SUB, SUB)],
                                  self.a_sem.at[slot]).start()
            b_slot, q = rights[e]
            if full:
                for f, width in enumerate((p.half, nt * TILE - p.half)):
                    pltpu.make_async_copy(src.at[b_slot, p.rows(q), pl.ds(p.base(f), width)],
                                          self.b_buf.at[slot, pl.ds(e * SUB, SUB), pl.ds(f * p.half, width)],
                                          self.b_sem.at[slot]).start()
            else:
                for g in range(2 * nt):
                    pltpu.make_async_copy(src.at[b_slot, p.rows(q), p.cols(2 * tile0 + g)],
                                          self.b_buf.at[slot, pl.ds(e * SUB, SUB), pl.ds(g * SUB, SUB)],
                                          self.b_sem.at[slot]).start()

    def ready(self, src, slot, tile0, nt, ones):
        k = 2 * SUB
        pltpu.make_async_copy(src.at[0, :, pl.ds(0, k)], self.a_buf.at[slot], self.a_sem.at[slot]).wait()
        pltpu.make_async_copy(src.at[0, pl.ds(0, k), pl.ds(0, nt * TILE)],
                              self.b_buf.at[slot, :, pl.ds(0, nt * TILE)], self.b_sem.at[slot]).wait()
        for e, r in ones:
            @pl.when((r >= 2 * tile0) & (r < 2 * (tile0 + nt)))
            def _():
                where = pl.ds(pl.multiple_of((r - 2 * tile0) * SUB, SUB), SUB)
                self.b_buf[slot, e * SUB:(e + 1) * SUB, where] += self.eye[...]

    def product(self, slot, t, rows):
        where = pl.ds(pl.multiple_of(t * TILE, TILE), TILE)
        return jnp.dot(self.a_buf[slot, rows, :], self.b_buf[slot, :, where], preferred_element_type=jnp.float32)

    def step(self, slot, which, tile0, nt, init):
        blocks = [pl.ds(m, BLOCK) for m in range(0, self.a_buf.shape[1], BLOCK)]

        def add(t):
            for rows in blocks:
                before = self.acc[which, tile0 + t, rows, :]
                if init is not False:
                    before = jnp.where(init, 0.0, before)
                self.acc[which, tile0 + t, rows, :] = before + self.product(slot, t, rows)

        if nt > 1:
            @pl.loop(0, nt // 2)
            def _(g):
                add(2 * g)
                add(2 * g + 1)
        if nt % 2:
            add(nt - 1)

    def finish(self, slot, which, tile0, nt, dst, before, after):
        p = self.place
        ring_size, part = self.ring.shape[0], self.ring.shape[1]
        parts = self.a_buf.shape[1] // part

        def put(u):
            t, h, s = u // parts, u % parts, u % ring_size
            rows = pl.ds(pl.multiple_of(h * part, part), part)
            return [pltpu.make_async_copy(self.ring.at[s, :, pl.ds(e * SUB, SUB)],
                                          dst.at[rows, p.cols(2 * (tile0 + t) + e)], self.out_sem.at[s, e])
                    for e in range(2)]

        def put_wait(u):
            for c in put(u):
                c.wait()

            @pl.when(u % parts == parts - 1)
            def _():
                after(tile0 + u // parts)

        n = nt * parts
        before()

        def body(u, carry):
            s = lax.rem(u, ring_size)

            @pl.when(u >= ring_size)
            def _():
                put_wait(u - ring_size)

            t = u // parts
            base = (u % parts) * part
            for m in range(0, part, BLOCK):
                rows = pl.ds(pl.multiple_of(base + m, BLOCK), BLOCK)
                total = self.acc[which, tile0 + t, rows, :] + self.product(slot, t, rows)
                self.ring[s, m:m + BLOCK, :] = jnp.minimum(total, 1.0).astype(jnp.bfloat16)
            for c in put(u):
                c.start()
            return carry

        lax.fori_loop(0, n, body, 0)

        def tail(u, carry):
            put_wait(u)
            return carry

        lax.fori_loop(max(0, n - ring_size), n, tail, 0)

    def gemm(self, src, n, load, which, tile0, nt, first, ones, final=None):
        load(0, 0)

        def body(k, carry):
            slot = lax.rem(k, 2)

            @pl.when(k + 1 < n)
            def _():
                load(k + 1, 1 - slot)

            self.ready(src, slot, tile0, nt, ones(k))
            self.step(slot, which, tile0, nt, (k == 0) if first else False)
            return carry

        lax.fori_loop(0, n - 1 if final else n, body, 0)
        if final:
            slot = (n - 1) % 2
            dst, after = final
            self.finish(slot, which, tile0, nt, dst, lambda: self.ready(src, slot, tile0, nt, ones(n - 1)), after)


def nothing(*args):
    return None


def square_tiles(engine, src, tile0, nt, full, final, arrive=nothing):
    p = engine.place

    def load(k, slot):
        arrive(k)
        f, q = k // p.per, k % p.per
        engine.load(src, slot, [(OWN, k), (HORI, k)],
                    [(p.right_slot(0, 0, f), q), (p.right_slot(0, 1, f), q)], tile0, nt, full)

    engine.gemm(src, 2 * p.per, load, 0, tile0, nt, True, lambda k: [(0, k)], final)


def pair_kernel(in_ref, new, work, acc, a_buf, b_buf, ring, eye, a_sem, b_sem, out_sem, x_s, x_r, y_s, y_r, m_s, m_r, mx_s,
                mx_r, my_s, my_r, dx_s, dx_r, dy_s, dy_r, md_s, md_r, n_s, n_r, ny_s, ny_r,
                ex_s, ex_r, ey_s, ey_r):
    rows, cols = in_ref.shape
    p = Place(cols // 2)
    per, half = p.per, p.half
    count = 2 * per
    tiles = cols // TILE
    kept = tiles - 1
    top = pl.ds(0, rows // 2)
    low = pl.ds(rows // 2, rows // 2)
    x_dev = {'col': 1 - p.col}
    y_dev = {'depth': 1 - p.depth}
    m_dev = {'row': 1 - p.row}
    engine = Engine(p, a_buf, b_buf, acc, ring, eye, a_sem, b_sem, out_sem)

    barrier = pltpu.get_barrier_semaphore()
    for dev in (x_dev, y_dev, m_dev):
        pl.semaphore_signal(barrier, inc=1, device_id=dev, device_id_type=MESH)
    pl.semaphore_wait(barrier, 3)

    def remote(src, dst, s_sem, r_sem, dev):
        return pltpu.make_async_remote_copy(src_ref=src, dst_ref=dst, send_sem=s_sem, recv_sem=r_sem, device_id=dev,
                                            device_id_type=MESH)

    def send_x(src, s, r):
        return remote(src.at[:, p.cols(r)], work.at[s, HORI, :, p.cols(r)], x_s.at[r], x_r.at[r], x_dev)

    def send_mate(src, s, r):
        return remote(src.at[:, p.cols(r)], work.at[s, MATE, :, p.cols(r)], m_s.at[r], m_r.at[r], m_dev)

    def send_y_near(src, s, q):
        return remote(src.at[:, p.cols(q)], work.at[s, VERT, :, p.cols(q)], y_s.at[q], y_r.at[q], y_dev)

    def send_y_far(src, s, q):
        far = pl.ds(p.base(1), half)
        return remote(src.at[p.rows(q), far], work.at[s, VERT, p.rows(q), far], y_s.at[per + q], y_r.at[per + q], y_dev)

    def pass_x(s, r):
        return remote(work.at[s, HORI, :, p.cols(r)], work.at[s, MATE_HORI, :, p.cols(r)], mx_s.at[r], mx_r.at[r], m_dev)

    def pass_y_near(s, q):
        return remote(work.at[s, VERT, :, p.cols(per + q)], work.at[s, MATE_VERT, :, p.cols(per + q)], my_s.at[q],
                      my_r.at[q], m_dev)

    def pass_y_far(s, q):
        near = pl.ds(p.base(0), half)
        return remote(work.at[s, VERT, p.rows(q), near], work.at[s, MATE_VERT, p.rows(q), near], my_s.at[per + q],
                      my_r.at[per + q], m_dev)

    def pass_diag(s, r):
        return remote(work.at[s, DIAG, :, p.cols(r)], work.at[s, MATE_DIAG, :, p.cols(r)], md_s.at[r], md_r.at[r], m_dev)

    def forward_x(s, r):
        return remote(work.at[s, VERT, top, p.cols(r)], work.at[s, DIAG, top, p.cols(r)], dx_s.at[r], dx_r.at[r], x_dev)

    def forward_y(s, r):
        mine = p.cols(lax.rem(r + per, count))
        return remote(work.at[s, HORI, low, mine], work.at[s, DIAG, low, mine], dy_s.at[r], dy_r.at[r], y_dev)

    def send_new(t):
        return remote(new.at[OWN], new.at[MATE], n_s.at[0], n_r.at[0], m_dev)

    def send_new_y(r):
        return remote(new.at[VERT, :, p.cols(r)], new.at[MATE_VERT, :, p.cols(r)], ny_s.at[r], ny_r.at[r], m_dev)

    def edge_x(e):
        where = p.cols(2 * kept + e)
        return remote(new.at[OWN, :, where], new.at[HORI, :, where], ex_s.at[e], ex_r.at[e], x_dev)

    def edge_y(e):
        where = p.cols(2 * kept + e - per)
        return remote(new.at[OWN, :, where], new.at[VERT, :, where], ey_s.at[e], ey_r.at[e], y_dev)

    def exchange(s, carry):
        src = work.at[s]

        @pl.when(s == 0)
        def _():
            for r in range(count):
                send_x(in_ref, 0, r).start()
                if r < per:
                    send_y_near(in_ref, 0, r).start()
                else:
                    send_y_far(in_ref, 0, r - per).start()
                send_mate(in_ref, 0, r).start()

            @pl.loop(0, tiles)
            def _(t):
                where = pl.ds(pl.multiple_of(t * TILE, TILE), TILE)
                for h, part in enumerate((top, low)):
                    load = pltpu.make_async_copy(in_ref.at[part, where], ring.at[h], out_sem.at[h, 0])
                    load.start()
                    load.wait()
                    store = pltpu.make_async_copy(ring.at[h], work.at[0, OWN, part, where], out_sem.at[h, 0])
                    store.start()
                    store.wait()

        @pl.loop(0, count)
        def _(r):
            send_mate(work.at[s, OWN], s, r).wait_recv()

        def own_load(f, q, slot):
            engine.load(src, slot, [(OWN, f * per + q), (HORI, f * per + q)],
                        [(p.right_slot(0, 0, f), q), (p.right_slot(0, 1, f), q)], 0, tiles, True)

        def near_arrive(q, slot):
            send_x(work.at[s, OWN], s, q).wait_recv()
            pass_x(s, q).start()
            own_load(0, q, slot)
            send_y_near(work.at[s, OWN], s, q).wait_recv()
            pass_y_near(s, q).start()
            pass_x(s, q).wait_recv()
            pass_y_near(s, q).wait_recv()

        engine.gemm(src, per, near_arrive, 0, 0, tiles, True, lambda k: [(0, k)])

        def hori(tile0, nt, f, final):
            def load(k, slot):
                engine.load(src, slot, [(OWN, f * per + k), (HORI, f * per + k)],
                            [(p.right_slot(HORI, 0, f), k), (p.right_slot(HORI, 1, f), k)], tile0, nt, False)

            engine.gemm(src, per, load, 1, tile0, nt, f == 0, lambda k: [(1, f * per + k)], final)

        hori_final = (new.at[HORI], nothing)

        def far_arrive(q):
            send_x(work.at[s, OWN], s, per + q).wait_recv()
            pass_x(s, per + q).start()
            forward_y(s, q).start()
            send_y_far(work.at[s, OWN], s, q).wait_recv()
            pass_y_far(s, q).start()

        def far_half(q, carry):
            far_arrive(q)

            @pl.when(q == per // 2)
            def _():
                @pl.loop(0, per)
                def _(r):
                    forward_x(s, r).start()

            pass_x(s, per + q).wait_recv()
            pass_y_far(s, q).wait_recv()
            own_load(1, q, 0)
            engine.ready(src, 0, 0, tiles, [(0, per + q)])
            engine.step(0, 0, 0, tiles, False)

            @pl.when(lax.rem(q, 2) == 0)
            def _():
                hori(q, 2, 0, None)

            return carry

        lax.fori_loop(0, per - 1, far_half, 0)
        far_arrive(per - 1)

        @pl.loop(per, count)
        def _(r):
            forward_x(s, r).start()
            forward_y(s, r).start()

        pass_x(s, count - 1).wait_recv()
        pass_y_far(s, per - 1).wait_recv()
        own_load(1, per - 1, 0)
        engine.finish(0, 0, 0, tiles, new.at[OWN], lambda: engine.ready(src, 0, 0, tiles, [(0, count - 1)]), nothing)
        send_new(0).start()
        for e in range(2):
            edge_x(e).start()
            edge_y(e).start()

        def vert_home(k, slot):
            engine.load(src, slot, [(VERT, k), (VERT, per + k)], [(p.right_slot(0, 0, 0), k), (p.right_slot(0, 0, 1), k)],
                        0, kept, True)

        engine.gemm(src, per, vert_home, 0, 0, kept, True, lambda k: [(0, k), (1, per + k)])

        def vert_away(first):
            def load(k, slot):
                r = first + 2 * k
                engine.load(src, slot, [(DIAG, r), (DIAG, r + 1)],
                            [(p.right_slot(0, 1, r // per), r % per), (p.right_slot(0, 1, (r + 1) // per), (r + 1) % per)],
                            0, kept, True)

            return load

        def diag_arrive(r, carry):
            forward_x(s, r).wait_recv()
            forward_y(s, r).wait_recv()

            @pl.when(r < 2 * kept)
            def _():
                pass_diag(s, r).start()

            return carry

        def diag_mate(r, carry):
            pass_diag(s, r).wait_recv()
            return carry

        def diag_group(g, carry):
            first = 4 * g
            lax.fori_loop(first, first + 4, diag_arrive, 0)
            engine.gemm(src, 2, vert_away(first), 0, 0, kept, False, lambda k: [])
            lax.fori_loop(first, first + 4, diag_mate, 0)
            hori(2 * g, 2, 1, hori_final)
            return carry

        lax.fori_loop(0, per // 2, diag_group, 0)
        lax.fori_loop(count - 2, count, diag_arrive, 0)
        vert_away(count - 2)(0, 0)

        def new_y(t):
            for e in range(2):
                send_new_y(2 * t + e).start()

        engine.finish(0, 0, 0, kept, new.at[VERT], lambda: engine.ready(src, 0, 0, kept, []), new_y)
        send_new(0).wait_recv()

        def drain(r, carry):
            own = work.at[s, OWN]
            for copy in (send_x(own, s, r), send_mate(own, s, r), pass_x(s, r), forward_x(s, r), forward_y(s, r)):
                copy.wait_send()

            @pl.when(r < 2 * kept)
            def _():
                pass_diag(s, r).wait_send()

            @pl.when(r < per)
            def _():
                send_y_near(own, s, r).wait_send()
                send_y_far(own, s, r).wait_send()
                pass_y_near(s, r).wait_send()
                pass_y_far(s, r).wait_send()

            return carry

        lax.fori_loop(0, count, drain, 0)

        def new_y_arrive():
            def body(r, carry):
                send_new_y(r).wait_recv()
                return carry

            lax.fori_loop(0, count, body, 0)
            for e in range(2):
                edge_x(e).wait_recv()

        def all_sent():
            send_new(0).wait_send()
            for e in range(2):
                edge_x(e).wait_send()
                edge_y(e).wait_send()

            def sent(r, carry):
                send_new_y(r).wait_send()
                return carry

            lax.fori_loop(0, count, sent, 0)

        for e in range(2):
            edge_y(e).wait_recv()
            send_new_y(2 * kept + e).start()

        @pl.when(s == 0)
        def _():
            fresh = work.at[1, OWN]

            def go(t):
                for e in range(2):
                    r = 2 * t + e
                    send_x(fresh, 1, r).start()
                    send_mate(fresh, 1, r).start()

                    @pl.when(r < per)
                    def _():
                        send_y_near(fresh, 1, r).start()

            def arrive(k):
                if isinstance(k, int):
                    return

                @pl.when(k == per)
                def _():
                    new_y_arrive()

            square_tiles(engine, new, 0, 1, False, (fresh, go), arrive)

            def group(g, carry):
                square_tiles(engine, new, 1 + 2 * g, 2, False, (fresh, go))
                return carry

            lax.fori_loop(0, tiles // 2, group, 0)
            all_sent()
            for q in range(per):
                send_y_far(fresh, 1, q).start()

        @pl.when(s > 0)
        def _():
            new_y_arrive()
            all_sent()

        return carry

    lax.fori_loop(0, SQUARINGS // 2, exchange, 0)


def last_kernel(new, out_ref, acc, a_buf, b_buf, ring, eye, a_sem, b_sem, out_sem):
    cols = out_ref.shape[1]
    p = Place(cols // 2)
    engine = Engine(p, a_buf, b_buf, acc, ring, eye, a_sem, b_sem, out_sem)
    square_tiles(engine, new, 0, cols // TILE, True, (out_ref, nothing))


def solution(mesh):
    def run(slab):
        rows, cols = slab.shape
        count = cols // SUB
        tiles = cols // TILE
        dma = pltpu.SemaphoreType.DMA
        hbm = pl.BlockSpec(memory_space=pl.ANY)

        def scratch(n_acc):
            return [
                pltpu.VMEM((n_acc, tiles, rows, TILE), jnp.float32),
                pltpu.VMEM((2, rows, 2 * SUB), jnp.bfloat16),
                pltpu.VMEM((2, 2 * SUB, cols), jnp.bfloat16),
                pltpu.VMEM((RING, rows // 2, TILE), jnp.bfloat16),
                pltpu.VMEM((SUB, SUB), jnp.bfloat16),
                dma((2,)), dma((2,)), dma((RING, 2)),
            ]

        new, _ = pl.pallas_call(
            pair_kernel,
            out_shape=(jax.ShapeDtypeStruct((5, rows, cols), jnp.bfloat16),
                       jax.ShapeDtypeStruct((2, 8, rows, cols), jnp.bfloat16)),
            in_specs=[hbm],
            out_specs=(hbm, hbm),
            scratch_shapes=scratch(2) + [dma((count,)) for _ in range(16)] + [dma((1,)), dma((1,)), dma((count,)),
                                                                              dma((count,))] + [dma((2,))] * 4,
            compiler_params=pltpu.CompilerParams(collective_id=0, has_side_effects=True, vmem_limit_bytes=67_000_000),
            name='reach_pairs',
        )(slab)
        return pl.pallas_call(
            last_kernel,
            out_shape=jax.ShapeDtypeStruct((rows, cols), jnp.bfloat16),
            in_specs=[hbm],
            out_specs=hbm,
            scratch_shapes=scratch(1),
            compiler_params=pltpu.CompilerParams(vmem_limit_bytes=67_000_000),
            name='reach_last',
        )(new)

    layout = P(('row', 'depth'), 'col')
    return jax.shard_map(run, mesh=mesh, in_specs=(layout,), out_specs=layout, check_vma=False)
```

time: 5940 us -> 1100 us (0.19); the launches traced: 5830 us -> 1100 us
  waiting for transfers between devices: 3780 us -> 0 us
  starting transfers between devices: 1550 us -> 0 us
  Pallas kernels: 0 us -> 1100 us
  matrix products: 413 us -> 0 us
  other arithmetic: 70 us -> 0 us
    unnamed x12 -> x0, waiting for transfers between devices: 2580 us -> none
    ppermute x8 -> x0, starting transfers between devices: 1550 us -> none  [the longest x4 776 us: local_squarings(): b_block = lax.ppermute(full_block, all_axes, b_skew)]
    all_gather x4 -> x0, waiting for transfers between devices: 1200 us -> none  [local_squarings(): full_block = lax.all_gather(row_slab, 'depth', axis=0, tiled=True)]
    pallas_call x0 -> x2, Pallas kernels: none -> 1100 us  [the longest x1 995 us: run(): pl.pallas_call(pair_kernel, out_shape=(jax.ShapeDtypeStruct((5, rows, col...]
    dot_general x4 -> x0, matrix products: 413 us -> none  [local_squarings(): jnp.dot(window[slot_id], b_block, preferred_element_type=jnp.float32)]
    convert_element_type x4 -> x0, other arithmetic: 70 us -> none  [local_squarings(): jnp.minimum(reduced + row_slab.astype(jnp.float32), 1.0)]
  transfers between devices with their start and end apart: 16 -> 0, of which waited for: 8 -> 0; matrix products, arithmetic and copies ran while one was open for 0% -> 0% of each run, Pallas kernels for 0% -> 0%
where the time goes in v2:
time: 1100 us
  Pallas kernels  1100 us (100%)
    pallas_call x1, Pallas kernels, run(): pl.pallas_call(pair_kernel, out_shape=(jax.ShapeDtypeStruct((5, rows, col...  995 us
    pallas_call x1, Pallas kernels, run(): pl.pallas_call(last_kernel, out_shape=jax.ShapeDtypeStruct((rows, cols),...  109 us

profile of v2, /device:TPU:0, one launch (start us, length us, event | category | flops | bytes accessed | tf_op | source)
XLA Modules:
  0.0 1103.9 jit_solution(2169242106638034565)
XLA Ops:
  0.0 994.7 %reach_pairs.1 = (bf16[5,1792,3584]{2,1,0:T(8,128)(2,1)}, bf16[2,8,1792,3584]{3,2,1,0:T(8,128)(2,1)}) custom-call(bf16[1792,3584]{1,0:T(8,128)(2,1)} %in_ref.1), custom_call_target="tpu_custom_call" | custom-call | tf_op jit(solution)/shard_map/reach_pairs/pallas_call | solution.py:520
  994.7 109.1 %reach_last.1 = bf16[1792,3584]{1,0:T(8,128)(2,1)} custom-call(bf16[5,1792,3584]{2,1,0:T(8,128)(2,1)} %get-tuple-element.6.new), custom_call_target="tpu_custom_call" | custom-call | tf_op jit(solution)/shard_map/reach_last/pallas_call | solution.py:531

commit v3 on v2

--- a/solution.py
+++ b/solution.py
@@ -10,7 +10,7 @@
 SQUARINGS = 4
 SUB = 256
 TILE = 512
-BLOCK = 448
+BLOCK = 224
 RING = 3
 MESH = pl.DeviceIdType.MESH
 OWN, MATE, VERT, MATE_VERT, HORI, MATE_HORI, DIAG, MATE_DIAG = range(8)
@@ -148,15 +148,21 @@
 
         lax.fori_loop(max(0, n - ring_size), n, tail, 0)
 
-    def gemm(self, src, n, load, which, tile0, nt, first, ones, final=None):
-        load(0, 0)
+    def gemm(self, src, n, load, which, tile0, nt, first, ones, final=None, start=0, loaded=False, following=None):
+        if not loaded:
+            load(0, start)
 
         def body(k, carry):
-            slot = lax.rem(k, 2)
+            slot = (start + k) % 2
 
             @pl.when(k + 1 < n)
             def _():
                 load(k + 1, 1 - slot)
+
+            if following and not final:
+                @pl.when(k + 1 == n)
+                def _():
+                    following(1 - slot)
 
             self.ready(src, slot, tile0, nt, ones(k))
             self.step(slot, which, tile0, nt, (k == 0) if first else False)
@@ -164,25 +170,33 @@
 
         lax.fori_loop(0, n - 1 if final else n, body, 0)
         if final:
-            slot = (n - 1) % 2
+            slot = (start + n - 1) % 2
             dst, after = final
-            self.finish(slot, which, tile0, nt, dst, lambda: self.ready(src, slot, tile0, nt, ones(n - 1)), after)
+
+            def before():
+                if following:
+                    following(1 - slot)
+                self.ready(src, slot, tile0, nt, ones(n - 1))
+
+            self.finish(slot, which, tile0, nt, dst, before, after)
 
 
 def nothing(*args):
     return None
 
 
-def square_tiles(engine, src, tile0, nt, full, final, arrive=nothing):
+def square_load(engine, src, k, slot, tile0, nt, full):
     p = engine.place
-
+    f, q = k // p.per, k % p.per
+    engine.load(src, slot, [(OWN, k), (HORI, k)], [(p.right_slot(0, 0, f), q), (p.right_slot(0, 1, f), q)], tile0, nt, full)
+
+
+def square_tiles(engine, src, tile0, nt, full, final, arrive=nothing, **chain):
     def load(k, slot):
         arrive(k)
-        f, q = k // p.per, k % p.per
-        engine.load(src, slot, [(OWN, k), (HORI, k)],
-                    [(p.right_slot(0, 0, f), q), (p.right_slot(0, 1, f), q)], tile0, nt, full)
-
-    engine.gemm(src, 2 * p.per, load, 0, tile0, nt, True, lambda k: [(0, k)], final)
+        square_load(engine, src, k, slot, tile0, nt, full)
+
+    engine.gemm(src, 2 * engine.place.per, load, 0, tile0, nt, True, lambda k: [(0, k)], final, **chain)
 
 
 def pair_kernel(in_ref, new, work, acc, a_buf, b_buf, ring, eye, a_sem, b_sem, out_sem, x_s, x_r, y_s, y_r, m_s, m_r, mx_s,
@@ -300,67 +314,83 @@
             pass_x(s, q).wait_recv()
             pass_y_near(s, q).wait_recv()
 
-        engine.gemm(src, per, near_arrive, 0, 0, tiles, True, lambda k: [(0, k)])
-
-        def hori(tile0, nt, f, final):
+        def hori(tile0, nt, f, final, start, following, loaded=True):
+            engine.gemm(src, per, hori_load(tile0, nt, f), 1, tile0, nt, f == 0, lambda k: [(1, f * per + k)], final,
+                        start, loaded, following)
+
+        def hori_load(tile0, nt, f):
             def load(k, slot):
                 engine.load(src, slot, [(OWN, f * per + k), (HORI, f * per + k)],
                             [(p.right_slot(HORI, 0, f), k), (p.right_slot(HORI, 1, f), k)], tile0, nt, False)
 
-            engine.gemm(src, per, load, 1, tile0, nt, f == 0, lambda k: [(1, f * per + k)], final)
+            return load
 
         hori_final = (new.at[HORI], nothing)
 
-        def far_arrive(q):
+        def far_prepare(q, slot):
             send_x(work.at[s, OWN], s, per + q).wait_recv()
             pass_x(s, per + q).start()
             forward_y(s, q).start()
             send_y_far(work.at[s, OWN], s, q).wait_recv()
             pass_y_far(s, q).start()
 
-        def far_half(q, carry):
-            far_arrive(q)
-
             @pl.when(q == per // 2)
             def _():
                 @pl.loop(0, per)
                 def _(r):
                     forward_x(s, r).start()
 
+            @pl.when(q == per - 1)
+            def _():
+                @pl.loop(per, count)
+                def _(r):
+                    forward_x(s, r).start()
+                    forward_y(s, r).start()
+
             pass_x(s, per + q).wait_recv()
             pass_y_far(s, q).wait_recv()
-            own_load(1, q, 0)
-            engine.ready(src, 0, 0, tiles, [(0, per + q)])
-            engine.step(0, 0, 0, tiles, False)
-
-            @pl.when(lax.rem(q, 2) == 0)
-            def _():
-                hori(q, 2, 0, None)
+            own_load(1, q, slot)
+
+        engine.gemm(src, per, near_arrive, 0, 0, tiles, True, lambda k: [(0, k)],
+                    following=lambda slot: far_prepare(jnp.int32(0), slot))
+
+        def far_half(q, carry):
+            slot = 1 - (q // 2) % 2
+            even = lax.rem(q, 2) == 0
+
+            @pl.when(even)
+            def _():
+                hori_load(q, 2, 0)(0, 1 - slot)
+
+            @pl.when(jnp.logical_not(even))
+            def _():
+                far_prepare(q + 1, 1 - slot)
+
+            engine.ready(src, slot, 0, tiles, [(0, per + q)])
+            engine.step(slot, 0, 0, tiles, False)
+
+            @pl.when(even)
+            def _():
+                hori(q, 2, 0, None, 1 - slot, lambda after: far_prepare(q + 1, after))
 
             return carry
 
         lax.fori_loop(0, per - 1, far_half, 0)
-        far_arrive(per - 1)
-
-        @pl.loop(per, count)
-        def _(r):
-            forward_x(s, r).start()
-            forward_y(s, r).start()
-
-        pass_x(s, count - 1).wait_recv()
-        pass_y_far(s, per - 1).wait_recv()
-        own_load(1, per - 1, 0)
-        engine.finish(0, 0, 0, tiles, new.at[OWN], lambda: engine.ready(src, 0, 0, tiles, [(0, count - 1)]), nothing)
+        last = 1 - ((per - 1) // 2) % 2
+
+        def own_before():
+            vert_home(0, 1 - last)
+            engine.ready(src, last, 0, tiles, [(0, count - 1)])
+
+        def vert_home(k, slot):
+            engine.load(src, slot, [(VERT, k), (VERT, per + k)], [(p.right_slot(0, 0, 0), k), (p.right_slot(0, 0, 1), k)],
+                        0, kept, True)
+
+        engine.finish(last, 0, 0, tiles, new.at[OWN], own_before, nothing)
         send_new(0).start()
         for e in range(2):
             edge_x(e).start()
             edge_y(e).start()
-
-        def vert_home(k, slot):
-            engine.load(src, slot, [(VERT, k), (VERT, per + k)], [(p.right_slot(0, 0, 0), k), (p.right_slot(0, 0, 1), k)],
-                        0, kept, True)
-
-        engine.gemm(src, per, vert_home, 0, 0, kept, True, lambda k: [(0, k), (1, per + k)])
 
         def vert_away(first):
             def load(k, slot):
@@ -385,23 +415,33 @@
             pass_diag(s, r).wait_recv()
             return carry
 
+        def diag_next(first, slot):
+            lax.fori_loop(first, jnp.minimum(first + 4, count), diag_arrive, 0)
+            vert_away(first)(0, slot)
+
+        engine.gemm(src, per, vert_home, 0, 0, kept, True, lambda k: [(0, k), (1, per + k)], None, 1 - last, True,
+                    lambda slot: diag_next(jnp.int32(0), slot))
+
         def diag_group(g, carry):
             first = 4 * g
-            lax.fori_loop(first, first + 4, diag_arrive, 0)
-            engine.gemm(src, 2, vert_away(first), 0, 0, kept, False, lambda k: [])
-            lax.fori_loop(first, first + 4, diag_mate, 0)
-            hori(2 * g, 2, 1, hori_final)
+            slot = (last + g) % 2
+
+            def mate_next(after):
+                lax.fori_loop(first, first + 4, diag_mate, 0)
+                hori_load(2 * g, 2, 1)(0, after)
+
+            engine.gemm(src, 2, vert_away(first), 0, 0, kept, False, lambda k: [], None, slot, True, mate_next)
+            hori(2 * g, 2, 1, hori_final, slot, lambda after: diag_next(first + 4, after))
             return carry
 
         lax.fori_loop(0, per // 2, diag_group, 0)
-        lax.fori_loop(count - 2, count, diag_arrive, 0)
-        vert_away(count - 2)(0, 0)
 
         def new_y(t):
             for e in range(2):
                 send_new_y(2 * t + e).start()
 
-        engine.finish(0, 0, 0, kept, new.at[VERT], lambda: engine.ready(src, 0, 0, kept, []), new_y)
+        ending = (last + per // 2) % 2
+        engine.finish(ending, 0, 0, kept, new.at[VERT], lambda: engine.ready(src, ending, 0, kept, []), new_y)
         send_new(0).wait_recv()
 
         def drain(r, carry):
@@ -471,10 +511,16 @@
                 def _():
                     new_y_arrive()
 
-            square_tiles(engine, new, 0, 1, False, (fresh, go), arrive)
+            square_tiles(engine, new, 0, 1, False, (fresh, go), arrive,
+                         following=lambda slot: square_load(engine, new, 0, slot, 1, 2, False))
 
             def group(g, carry):
-                square_tiles(engine, new, 1 + 2 * g, 2, False, (fresh, go))
+                def following(slot):
+                    @pl.when(g + 1 < tiles // 2)
+                    def _():
+                        square_load(engine, new, 0, slot, 3 + 2 * g, 2, False)
+
+                square_tiles(engine, new, 1 + 2 * g, 2, False, (fresh, go), loaded=True, following=following)
                 return carry
 
             lax.fori_loop(0, tiles // 2, group, 0)

time: 1100 us -> 1050 us (0.955)
  Pallas kernels: 1100 us -> 1050 us
    pallas_call x1, Pallas kernels: 995 us -> 940 us  [run(): pl.pallas_call(pair_kernel, out_shape=(jax.ShapeDtypeStruct((5, rows, col...]
where the time goes in v3:
time: 1050 us
  Pallas kernels  1050 us (100%)
    pallas_call x1, Pallas kernels, run(): pl.pallas_call(pair_kernel, out_shape=(jax.ShapeDtypeStruct((5, rows, col...  940 us
    pallas_call x1, Pallas kernels, run(): pl.pallas_call(last_kernel, out_shape=jax.ShapeDtypeStruct((rows, cols),...  109 us

profile of v3, /device:TPU:0, one launch (start us, length us, event | category | flops | bytes accessed | tf_op | source)
XLA Modules:
  0.0 1049.7 jit_solution(1814031042947489328)
XLA Ops:
  0.0 940.1 %reach_pairs.1 = (bf16[5,1792,3584]{2,1,0:T(8,128)(2,1)}, bf16[2,8,1792,3584]{3,2,1,0:T(8,128)(2,1)}) custom-call(bf16[1792,3584]{1,0:T(8,128)(2,1)} %in_ref.1), custom_call_target="tpu_custom_call" | custom-call | tf_op jit(solution)/shard_map/reach_pairs/pallas_call | solution.py:566
  940.1 109.5 %reach_last.1 = bf16[1792,3584]{1,0:T(8,128)(2,1)} custom-call(bf16[5,1792,3584]{2,1,0:T(8,128)(2,1)} %get-tuple-element.6.new), custom_call_target="tpu_custom_call" | custom-call | tf_op jit(solution)/shard_map/reach_last/pallas_call | solution.py:577

commit v4 on v3

--- a/solution.py
+++ b/solution.py
@@ -82,7 +82,7 @@
         where = pl.ds(pl.multiple_of(t * TILE, TILE), TILE)
         return jnp.dot(self.a_buf[slot, rows, :], self.b_buf[slot, :, where], preferred_element_type=jnp.float32)
 
-    def step(self, slot, which, tile0, nt, init):
+    def step(self, slot, which, tile0, nt, init, unrolled=False):
         blocks = [pl.ds(m, BLOCK) for m in range(0, self.a_buf.shape[1], BLOCK)]
 
         def add(t):
@@ -92,6 +92,10 @@
                     before = jnp.where(init, 0.0, before)
                 self.acc[which, tile0 + t, rows, :] = before + self.product(slot, t, rows)
 
+        if unrolled:
+            for t in range(nt):
+                add(t)
+            return
         if nt > 1:
             @pl.loop(0, nt // 2)
             def _(g):
@@ -148,7 +152,8 @@
 
         lax.fori_loop(max(0, n - ring_size), n, tail, 0)
 
-    def gemm(self, src, n, load, which, tile0, nt, first, ones, final=None, start=0, loaded=False, following=None):
+    def gemm(self, src, n, load, which, tile0, nt, first, ones, final=None, start=0, loaded=False, following=None,
+             unrolled=False):
         if not loaded:
             load(0, start)
 
@@ -165,7 +170,7 @@
                     following(1 - slot)
 
             self.ready(src, slot, tile0, nt, ones(k))
-            self.step(slot, which, tile0, nt, (k == 0) if first else False)
+            self.step(slot, which, tile0, nt, (k == 0) if first else False, unrolled)
             return carry
 
         lax.fori_loop(0, n - 1 if final else n, body, 0)
@@ -196,7 +201,7 @@
         arrive(k)
         square_load(engine, src, k, slot, tile0, nt, full)
 
-    engine.gemm(src, 2 * engine.place.per, load, 0, tile0, nt, True, lambda k: [(0, k)], final, **chain)
+    engine.gemm(src, 2 * engine.place.per, load, 0, tile0, nt, True, lambda k: [(0, k)], final, unrolled=full, **chain)
 
 
 def pair_kernel(in_ref, new, work, acc, a_buf, b_buf, ring, eye, a_sem, b_sem, out_sem, x_s, x_r, y_s, y_r, m_s, m_r, mx_s,
@@ -420,7 +425,7 @@
             vert_away(first)(0, slot)
 
         engine.gemm(src, per, vert_home, 0, 0, kept, True, lambda k: [(0, k), (1, per + k)], None, 1 - last, True,
-                    lambda slot: diag_next(jnp.int32(0), slot))
+                    lambda slot: diag_next(jnp.int32(0), slot), True)
 
         def diag_group(g, carry):
             first = 4 * g
@@ -430,7 +435,7 @@
                 lax.fori_loop(first, first + 4, diag_mate, 0)
                 hori_load(2 * g, 2, 1)(0, after)
 
-            engine.gemm(src, 2, vert_away(first), 0, 0, kept, False, lambda k: [], None, slot, True, mate_next)
+            engine.gemm(src, 2, vert_away(first), 0, 0, kept, False, lambda k: [], None, slot, True, mate_next, True)
             hori(2 * g, 2, 1, hori_final, slot, lambda after: diag_next(first + 4, after))
             return carry
 

time: 1050 us -> 1040 us (level)
  no operation moved by 1% of the time
where the time goes in v4:
time: 1040 us
  Pallas kernels  1040 us (100%)
    pallas_call x1, Pallas kernels, run(): pl.pallas_call(pair_kernel, out_shape=(jax.ShapeDtypeStruct((5, rows, col...  937 us
    pallas_call x1, Pallas kernels, run(): pl.pallas_call(last_kernel, out_shape=jax.ShapeDtypeStruct((rows, cols),...  103 us

profile of v4, /device:TPU:0, one launch (start us, length us, event | category | flops | bytes accessed | tf_op | source)
XLA Modules:
  0.0 1040.3 jit_solution(6582534171159676554)
XLA Ops:
  0.0 937.0 %reach_pairs.1 = (bf16[5,1792,3584]{2,1,0:T(8,128)(2,1)}, bf16[2,8,1792,3584]{3,2,1,0:T(8,128)(2,1)}) custom-call(bf16[1792,3584]{1,0:T(8,128)(2,1)} %in_ref.1), custom_call_target="tpu_custom_call" | custom-call | tf_op jit(solution)/shard_map/reach_pairs/pallas_call | solution.py:571
  937.0 103.1 %reach_last.1 = bf16[1792,3584]{1,0:T(8,128)(2,1)} custom-call(bf16[5,1792,3584]{2,1,0:T(8,128)(2,1)} %get-tuple-element.6.new), custom_call_target="tpu_custom_call" | custom-call | tf_op jit(solution)/shard_map/reach_last/pallas_call | solution.py:582
